TPU v7x, 32 devices: a whole 2x2x4 slice. The times are simulated.
32 devices in a mesh: dp: 2 (over x), tp: 4 (over z), sq: 4 (over y, core).
Axes of the slice: x: 2, y: 2, z: 4, core: 2. Of those that a mesh axis runs over, the one named last changes fastest.
Arguments:
- hidden: bfloat16 [512, 2048], P('dp'), parts along dimension 0
- cache_lens: int32 [512], P('dp'), parts along dimension 0
- k_cache: bfloat16 [512, 1024, 128], P('dp', 'sq'), parts along dimension 0
- v_cache: bfloat16 [512, 1024, 128], P('dp', 'sq'), parts along dimension 0
- ln_gain: float32 [2048], replicated
- ln_bias: float32 [2048], replicated
- w_query: bfloat16 [2048, 2048], P(None, 'tp')
- b_query: float32 [2048], P('tp')
- w_kv: bfloat16 [2048, 256], replicated
- b_kv: float32 [256], replicated
- w_out: bfloat16 [2048, 2048], P('tp')
- b_out: float32 [2048], replicated
Outputs:
- output 1: bfloat16 [512, 2048], P('dp'), parts along dimension 0
- output 2: bfloat16 [512, 1024, 128], P('dp', 'sq'), parts along dimension 0
- output 3: bfloat16 [512, 1024, 128], P('dp', 'sq'), parts along dimension 0
There are 2 independent parts. A program takes and returns all parts, laid end to end along the dimension named above; an argument that names none is the same for every part.
All inputs are finite; a program needn't handle non-finite values.
Results may differ from a plain program's by a relative error of at most 0.00347619.
Values sent between devices are 32-bit elements.
A program may use at most 1 GiB of HBM per device.

v0:
```python
import jax
import jax.numpy as jnp
from jax import lax
from jax.sharding import PartitionSpec as P


def layer_norm(x_rows, ln_gain, ln_bias):
    x_wide = x_rows.astype(jnp.float32)
    mean_val = jnp.mean(x_wide, axis=-1, keepdims=True)
    centered = x_wide - mean_val
    variance = jnp.mean(centered * centered, axis=-1, keepdims=True)
    normed = centered * lax.rsqrt(variance + 1e-5)
    return (normed * ln_gain + ln_bias).astype(jnp.bfloat16)


def solution(mesh):
    def local_step(hidden, cache_lens, k_cache, v_cache, ln_gain, ln_bias, w_query, b_query, w_kv, b_kv, w_out, b_out):
        batch, pos_local, head_dim = k_cache.shape
        heads_local = w_query.shape[1] // head_dim
        normed = layer_norm(hidden, ln_gain, ln_bias)
        query = (jnp.dot(normed, w_query, preferred_element_type=jnp.float32) + b_query).astype(jnp.bfloat16)
        query = query.reshape(batch, heads_local, head_dim)
        key_val = (jnp.dot(normed, w_kv, preferred_element_type=jnp.float32) + b_kv).astype(jnp.bfloat16)
        first_pos = lax.axis_index("sq") * pos_local
        positions = first_pos + lax.broadcasted_iota(jnp.int32, (1, pos_local), 1)
        at_slot = (positions == cache_lens[:, None])[:, :, None]
        key_new = jnp.where(at_slot, key_val[:, None, :head_dim], k_cache)
        val_new = jnp.where(at_slot, key_val[:, None, head_dim:], v_cache)
        scores = jnp.einsum("bnd,btd->bnt", query, key_new, preferred_element_type=jnp.float32) * (head_dim ** -0.5)
        valid = (positions <= cache_lens[:, None])[:, None, :]
        scores = jnp.where(valid, scores, -1e30)
        local_max = jnp.max(scores, axis=-1, keepdims=True)
        global_max = lax.pmax(local_max, "sq")
        weights = jnp.where(valid, jnp.exp(scores - global_max), 0.0)
        denominator = lax.psum(jnp.sum(weights, axis=-1, keepdims=True), "sq")
        numerator = lax.psum(jnp.einsum("bnt,btd->bnd", weights.astype(jnp.bfloat16), val_new, preferred_element_type=jnp.float32), "sq")
        attended = (numerator / denominator).astype(jnp.bfloat16).reshape(batch, heads_local * head_dim)
        part_sum = jnp.dot(attended, w_out, preferred_element_type=jnp.float32)
        projected = lax.psum(part_sum, "tp")
        out_hidden = (hidden.astype(jnp.float32) + projected + b_out).astype(jnp.bfloat16)
        return out_hidden, key_new, val_new

    cache_spec = P("dp", "sq", None)
    row_spec = P("dp", None)
    in_specs = (row_spec, P("dp"), cache_spec, cache_spec, P(None), P(None), P(None, "tp"), P("tp"), P(None, None), P(None), P("tp", None), P(None))
    out_specs = (row_spec, cache_spec, cache_spec)
    return jax.shard_map(local_step, mesh=mesh, in_specs=in_specs, out_specs=out_specs, check_vma=False)
```

profile of v0, /device:TPU:0, one launch (start us, length us, event | category | flops | bytes accessed | tf_op | source)
XLA Modules:
  0.0 206.5 jit_solution(11914610228819217753)
XLA Ops:
  7.2 0.0 copy-start
  7.2 0.0 copy-start.1
  7.2 0.0 copy-start.7
  7.2 0.0 copy-start.8
  7.2 0.0 all-reduce.3.cloned.1.call-start
  7.3 0.0 copy-start.6
  7.3 1.6 convert_reduce_fusion
  8.9 1.6 fusion.2
  10.5 0.0 copy-done.1
  10.6 0.0 copy-done.7
  10.6 0.0 copy-done.8
  10.6 0.0 copy-done.6
  10.6 0.0 copy-start.5
  10.6 0.0 copy-start.9
  10.6 1.4 fusion.10
  12.0 0.1 copy-done.5
  12.2 0.0 copy-done.9
  12.2 0.0 copy-start.4
  12.2 1.5 fusion.9
  13.7 1.0 reshape.85
  14.7 0.0 copy-done.4
  14.7 0.1 broadcast_compare_fusion.1
  14.8 23.3 %broadcast_select_fusion.1 = (bf16[256,256,128]{2,1,0:T(8,128)(2,1)}, bf16[256,256,128]{2,1,0:T(8,128)(2,1)}) fusion(bf16[256,256,128]{2,1,0:T(8,128)(2,1)} %param.14, pred[256,256]{1,0:T(8,128)(4,1)S(1)} %get-tuple-element.8, bf16[256,128]{1,0:T(8,128)(2,1)S(1)} %get-tuple-element.3, bf16[256,256,128]{2,1,0:T(8,128)(2,1)} %param.15, ...), kind=kLoop, calls=%fused_computation.1 | loop fusion | flops 16777216 | bytes 67305472 | tf_op jit(solution)/shard_map/jit(_where)/select_n | solution.py:27
  38.1 11.0 %fusion.25 = (f32[256,4]{1,0:T(8,128)}, f32[256,4,256]{2,1,0:T(4,128)S(1)}) fusion(bf16[256,4,128]{2,1,0:T(4,128)(2,1)S(1)} %reshape.85, bf16[256,256,128]{2,1,0:T(8,128)(2,1)} %get-tuple-element.5, pred[256,256]{1,0:T(8,128)(4,1)S(1)} %get-tuple-element.7), kind=kOutput, calls=%fused_computation.37 | convolution fusion | flops 67894272 | bytes 18157568 | tf_op jit(solution)/shard_map/bnd,btd->bnt/dot_general | solution.py:29
  49.1 15.0 %pmax.7 = f32[256,4]{1,0:T(8,128)S(1)} all-reduce(f32[256,4]{1,0:T(8,128)} %get-tuple-element.9), channel_id=1, replica_groups=mesh['dp'=2,'tp'=4,'sq'=4] {'sq'}, use_global_device_ids=true, to_apply=%region_3.4 | all-reduce | flops 1024 | bytes 8192 | tf_op jit(solution)/shard_map/pmax | solution.py:33
  64.1 8.9 %fusion.13 = f32[256,4,128]{2,1,0:T(4,128)} fusion(bf16[256,256,128]{2,1,0:T(8,128)(2,1)} %get-tuple-element.6, f32[256,4,256]{2,1,0:T(4,128)S(1)} %get-tuple-element.10, f32[256,4]{1,0:T(8,128)S(1)} %pmax.7, pred[256,256]{1,0:T(8,128)(4,1)S(1)} %get-tuple-element.7), kind=kOutput, calls=%fused_computation.22 | convolution fusion | flops 67895296 | bytes 18419712 | tf_op jit(solution)/shard_map/bnt,btd->bnd/dot_general | solution.py:36
  73.0 0.0 all-reduce.3.cloned.1.call-update
  73.0 0.0 all-reduce.5.cloned.1.call-start
  73.1 0.8 fusion.11
  73.9 12.0 %psum.22 = f32[256,4]{1,0:T(8,128)S(1)} all-reduce(f32[256,4]{1,0:T(8,128)S(1)} %fusion.11), channel_id=1, replica_groups=mesh['dp'=2,'tp'=4,'sq'=4] {'sq'}, use_global_device_ids=true, to_apply=%region_6.7 | all-reduce | flops 1024 | bytes 8192 | tf_op jit(solution)/shard_map/psum | solution.py:35
  85.9 21.6 %all-reduce.3.cloned.1.call-done = f32[256,4,128]{2,1,0:T(4,128)} async-done(((f32[256,4,128]{2,1,0:T(4,128)}), f32[256,4,128]{2,1,0:T(4,128)}) %all-reduce.3.cloned.1.call-update) | async-done | bytes 524304 | tf_op jit(solution)/shard_map/psum | solution.py:36
  107.5 1.4 divide_convert_fusion
  108.9 0.0 copy-done
  108.9 2.0 fusion.18
  111.0 0.0 copy-start.2
  111.0 0.0 copy-start.3
  111.0 0.0 all-reduce.5.cloned.1.call-update
  111.0 85.8 %all-reduce.5.cloned.1.call-done = f32[256,2048]{1,0:T(8,128)} async-done(((f32[256,2048]{1,0:T(8,128)}), f32[256,2048]{1,0:T(8,128)}) %all-reduce.5.cloned.1.call-update) | async-done | bytes 2097168 | tf_op jit(solution)/shard_map/psum | solution.py:39
  196.7 0.0 copy-done.2
  196.7 0.0 copy-done.3
  196.7 2.9 %fusion.7 = bf16[256,2048]{1,0:T(8,128)(2,1)} fusion(f32[256,2048]{1,0:T(8,128)} %all-reduce.5.cloned.1.call-done, bf16[256,2048]{1,0:T(8,128)(2,1)S(1)} %copy-done.2, f32[2048]{0:T(1024)S(1)} %copy-done.3), kind=kLoop, calls=%fused_computation.12 | loop fusion | flops 2097152 | bytes 4202496 | tf_op jit(solution)/shard_map/convert_element_type | solution.py:40
  (4 shorter events, 0.0 us)
Async XLA Ops:
  7.2 101.8 %copy-start = (bf16[512,2048]{1,0:T(8,128)(2,1)S(1)}, bf16[512,2048]{1,0:T(8,128)(2,1)}, u32[]{:S(2)}) copy-start(bf16[512,2048]{1,0:T(8,128)(2,1)} %param.22) | copy-start | bytes 6291460
  7.2 3.4 %copy-start.1 = (bf16[256,2048]{1,0:T(8,128)(2,1)S(1)}, bf16[256,2048]{1,0:T(8,128)(2,1)}, u32[]{:S(2)}) copy-start(bf16[256,2048]{1,0:T(8,128)(2,1)} %param.12) | copy-start | bytes 3145732
  7.2 3.4 %copy-start.7 = (f32[2048]{0:T(1024)S(1)}, f32[2048]{0:T(1024)}, u32[]{:S(2)}) copy-start(f32[2048]{0:T(1024)} %param.17) | copy-start | bytes 24580
  7.2 3.4 %copy-start.8 = (f32[2048]{0:T(1024)S(1)}, f32[2048]{0:T(1024)}, u32[]{:S(2)}) copy-start(f32[2048]{0:T(1024)} %param.16) | copy-start | bytes 24580
  7.2 100.3 %all-reduce.3.cloned.1.call-start = ((), (), s32[]{:S(2)}) async-start(), calls=%async_computation | async-start | bytes 1048576 | tf_op jit(solution)/shard_map/psum | solution.py:36
  7.3 3.3 %copy-start.6 = (bf16[2048,256]{1,0:T(8,128)(2,1)S(1)}, bf16[2048,256]{1,0:T(8,128)(2,1)}, u32[]{:S(2)}) copy-start(bf16[2048,256]{1,0:T(8,128)(2,1)} %param.20) | copy-start | bytes 3145732
  10.6 1.6 copy-start.5
  10.6 1.6 copy-start.9
  12.2 2.5 %copy-start.4 = (s32[256]{0:T(256)S(1)}, s32[256]{0:T(256)}, u32[]{:S(2)}) copy-start(s32[256]{0:T(256)} %param.13) | copy-start | bytes 3076
  73.0 123.7 %all-reduce.5.cloned.1.call-start = ((), (), s32[]{:S(2)}) async-start(), calls=%async_computation.1 | async-start | bytes 4194304 | tf_op jit(solution)/shard_map/psum | solution.py:39
  111.0 85.8 %copy-start.2 = (bf16[256,2048]{1,0:T(8,128)(2,1)S(1)}, bf16[256,2048]{1,0:T(8,128)(2,1)}, u32[]{:S(2)}) copy-start(bf16[256,2048]{1,0:T(8,128)(2,1)} %param.12) | copy-start | bytes 3145732
  111.0 85.8 %copy-start.3 = (f32[2048]{0:T(1024)S(1)}, f32[2048]{0:T(1024)}, u32[]{:S(2)}) copy-start(f32[2048]{0:T(1024)} %param.23) | copy-start | bytes 24580
Sparse Core Ops, SparseCore 0:
  73.2 34.3 all-reduce.2
  111.1 85.5 all-reduce.4
where the time goes:
time: 207 us; the launch traced here: 206 us
  waiting for transfers between devices  107 us (52%)
  other arithmetic  31.7 us (15%)
  blocking collectives  27 us (13%)
  matrix products  24.8 us (12%)
  between operations  14.2 us (7%)
    psum x1, waiting for transfers between devices, local_step(): projected = lax.psum(part_sum, 'tp')  85.8 us
    select_n x1, other arithmetic, local_step(): key_new = jnp.where(at_slot, key_val[:, None, :head_dim], k_cache)  23.3 us
    psum x1, waiting for transfers between devices, local_step(): lax.psum(jnp.einsum('bnt,btd->bnd', weights.astype(jnp.bfloat16), val_new...  21.6 us
    pmax x1, blocking collectives, local_step(): global_max = lax.pmax(local_max, 'sq')  15 us
    psum x1, blocking collectives, local_step(): denominator = lax.psum(jnp.sum(weights, axis=-1, keepdims=True), 'sq')  12 us
    dot_general x1, matrix products, local_step(): jnp.einsum('bnd,btd->bnt', query, key_new, preferred_element_type=jnp.flo...  11 us
    dot_general x1, matrix products, local_step(): jnp.einsum('bnt,btd->bnd', weights.astype(jnp.bfloat16), val_new, preferr...  8.91 us
  transfers between devices with their start and end apart: 2, of which 2 were waited for; matrix products, arithmetic and copies ran while one was open for 0% of the time, Pallas kernels for 0%

commit v1 on v0

v1 whole, which is shorter than its diff:
```python
import functools

import jax
import jax.numpy as jnp
from jax import lax
from jax.experimental import pallas as pl
from jax.experimental.pallas import tpu as pltpu
from jax.sharding import PartitionSpec as P

F32 = jnp.float32
BF16 = jnp.bfloat16
NEG = -1e30


def attend_kernel(
    pairs, lens_ref, x_hbm, gain_ref, bias_ref, wq_hbm, bq_ref, wkv_hbm, bkv_ref, k_hbm, v_hbm,
    k_out, v_out, acc_ref, ml_ref,
    x_buf, h_buf, wq_buf, wkv_buf, q_buf, kv_buf, s_buf, k_buf, v_buf, in_sem, k_sem, v_sem, ko_sem, vo_sem,
):
    batch, pos_local, dim = k_buf.shape
    heads = wq_buf.shape[1] // dim
    per = 2 * pairs
    chunks = batch // per
    rows = 2 * heads
    first_pos = lax.axis_index("sq") * pos_local
    scale = dim ** -0.5

    x_copy = pltpu.make_async_copy(x_hbm, x_buf, in_sem.at[0])
    kv_copy = pltpu.make_async_copy(wkv_hbm, wkv_buf, in_sem.at[1])
    q_copy = pltpu.make_async_copy(wq_hbm, wq_buf, in_sem.at[2])
    x_copy.start()
    kv_copy.start()
    q_copy.start()

    def span(ref, c):
        return ref.at[pl.ds(c * per, per)]

    def k_load(c):
        return pltpu.make_async_copy(span(k_hbm, c), span(k_buf, c), k_sem.at[c])

    def v_load(c):
        return pltpu.make_async_copy(span(v_hbm, c), span(v_buf, c), v_sem.at[c])

    def k_store(c):
        return pltpu.make_async_copy(span(k_buf, c), span(k_out, c), ko_sem.at[c])

    def v_store(c):
        return pltpu.make_async_copy(span(v_buf, c), span(v_out, c), vo_sem.at[c])

    @pl.loop(0, chunks)
    def _(c):
        k_load(c).start()
        v_load(c).start()

    x_copy.wait()
    block = 32

    @pl.loop(0, batch // block)
    def _(i):
        x = x_buf[pl.ds(i * block, block), :].astype(F32)
        mean = jnp.mean(x, axis=-1, keepdims=True)
        cen = x - mean
        var = jnp.mean(cen * cen, axis=-1, keepdims=True)
        h = cen * lax.rsqrt(var + 1e-5) * gain_ref[...] + bias_ref[...]
        h_buf[pl.ds(i * block, block), :] = h.astype(BF16)

    kv_copy.wait()
    kv = jnp.dot(h_buf[...], wkv_buf[...], preferred_element_type=F32) + bkv_ref[...]
    kv_buf[...] = kv.astype(BF16).astype(F32)
    q_copy.wait()
    for n0 in range(0, heads, 2):
        cols = slice(n0 * dim, (n0 + 2) * dim)
        q = jnp.dot(h_buf[...], wq_buf[:, cols], preferred_element_type=F32) + bq_ref[:, cols]
        q = q.astype(BF16).astype(F32)
        q_buf[pl.ds(n0, batch, stride=heads), :] = q[:, :dim]
        q_buf[pl.ds(n0 + 1, batch, stride=heads), :] = q[:, dim:]

    top = lax.broadcasted_iota(jnp.int32, (rows, dim), 0) < heads
    top2 = lax.broadcasted_iota(jnp.int32, (rows, pos_local), 0) < heads
    lane = lax.broadcasted_iota(jnp.int32, (rows, dim), 1)
    place = first_pos + lax.broadcasted_iota(jnp.int32, (rows, pos_local), 1)
    sub = lax.broadcasted_iota(jnp.int32, (16, dim), 0)

    def update_rows(c):
        fresh = kv_buf[pl.ds(pl.multiple_of(c * per, per), per), :]
        for j in range(per):
            b = c * per + j
            at = lens_ref[b] - first_pos
            base = pl.multiple_of(jnp.clip(at, 0, pos_local - 1) // 16 * 16, 16)
            hit = sub == at - base
            for buf, lo in ((k_buf, 0), (v_buf, dim)):
                new = jnp.broadcast_to(fresh[j:j + 1, lo:lo + dim], (16, dim))
                old = buf[b, pl.ds(base, 16), :].astype(F32)
                buf[b, pl.ds(base, 16), :] = jnp.where(hit, new, old).astype(BF16)

    def score(c):
        out = []
        for j in range(pairs):
            p = c * pairs + j
            q = q_buf[pl.ds(pl.multiple_of(p * rows, rows), rows), :]
            lhs = jnp.concatenate([jnp.where(top, q, 0.0), jnp.where(top, 0.0, q)], axis=1).astype(BF16)
            keys = jnp.concatenate([k_buf[2 * p], k_buf[2 * p + 1]], axis=1)
            s = lax.dot_general(lhs, keys, (((1,), (1,)), ((), ())), preferred_element_type=F32)
            out.append(s)
        return out

    def weigh(c, m_all, l_all):
        for j in range(pairs):
            p = c * pairs + j
            s = s_buf[j * rows:(j + 1) * rows, :] * scale
            last = jnp.where(top2, lens_ref[2 * p], lens_ref[2 * p + 1])
            valid = place <= last
            s = jnp.where(valid, s, NEG)
            m = jnp.max(s, axis=-1, keepdims=True)
            w = jnp.where(valid, jnp.exp(s - m), 0.0)
            total = jnp.sum(w, axis=-1, keepdims=True)
            vals = jnp.concatenate([v_buf[2 * p], v_buf[2 * p + 1]], axis=1)
            o = jnp.dot(w.astype(BF16), vals, preferred_element_type=F32)
            acc_ref[pl.ds(pl.multiple_of(p * rows, rows), rows), :] = jnp.where(top, o[:, :dim], o[:, dim:])
            m_all = jnp.where(lane == p, m, m_all)
            l_all = jnp.where(lane == p, total, l_all)
        return m_all, l_all

    def put_scores(out):
        for j, s in enumerate(out):
            s_buf[j * rows:(j + 1) * rows, :] = s

    def arrive(c):
        k_load(c).wait()
        v_load(c).wait()
        update_rows(c)

    def leave(c):
        k_store(c).start()
        v_store(c).start()

    arrive(0)
    put_scores(score(0))
    leave(0)
    zero = jnp.zeros((rows, dim), F32)

    def body(c, carry):
        arrive(c + 1)
        carry = weigh(c, *carry)
        put_scores(score(c + 1))
        leave(c + 1)
        return carry

    carry = lax.fori_loop(0, chunks - 1, body, (zero, zero))
    m_all, l_all = weigh(chunks - 1, *carry)
    ml_ref[:rows, :] = m_all
    ml_ref[rows:, :] = l_all

    @pl.loop(0, chunks)
    def _(c):
        k_store(c).wait()
        v_store(c).wait()


def attend(lens, x, gain, bias, wq, bq, wkv, bkv, k, v, pairs=8):
    batch, pos_local, dim = k.shape
    width = x.shape[1]
    heads = wq.shape[1] // dim
    chunks = batch // (2 * pairs)
    hbm = pl.BlockSpec(memory_space=pl.ANY)
    vmem = pl.BlockSpec(memory_space=pltpu.VMEM)
    dma = pltpu.SemaphoreType.DMA
    return pl.pallas_call(
        functools.partial(attend_kernel, pairs),
        out_shape=(
            jax.ShapeDtypeStruct(k.shape, k.dtype),
            jax.ShapeDtypeStruct(v.shape, v.dtype),
            jax.ShapeDtypeStruct((batch * heads, dim), F32),
            jax.ShapeDtypeStruct((4 * heads, dim), F32),
        ),
        in_specs=[pl.BlockSpec(memory_space=pltpu.SMEM), hbm, vmem, vmem, hbm, vmem, hbm, vmem, hbm, hbm],
        out_specs=(hbm, hbm, vmem, vmem),
        scratch_shapes=[
            pltpu.VMEM(x.shape, BF16),
            pltpu.VMEM(x.shape, BF16),
            pltpu.VMEM(wq.shape, BF16),
            pltpu.VMEM(wkv.shape, BF16),
            pltpu.VMEM((batch * heads, dim), F32),
            pltpu.VMEM((batch, 2 * dim), F32),
            pltpu.VMEM((pairs * 2 * heads, pos_local), F32),
            pltpu.VMEM(k.shape, BF16),
            pltpu.VMEM(v.shape, BF16),
            dma((3,)), dma((chunks,)), dma((chunks,)), dma((chunks,)), dma((chunks,)),
        ],
        compiler_params=pltpu.CompilerParams(vmem_limit_bytes=56 * 1024 * 1024),
        cost_estimate=pl.CostEstimate(flops=2 * 2**30, bytes_accessed=72 * 2**20, transcendentals=0),
        name="attend",
    )(lens, x, gain.reshape(1, width), bias.reshape(1, width), wq, bq.reshape(1, -1), wkv, bkv.reshape(1, -1), k, v)


def solution(mesh):
    def local_step(hidden, cache_lens, k_cache, v_cache, ln_gain, ln_bias, w_query, b_query, w_kv, b_kv, w_out, b_out):
        batch, pos_local, dim = k_cache.shape
        heads = w_query.shape[1] // dim
        key_new, val_new, acc, ml = attend(
            cache_lens, hidden, ln_gain, ln_bias, w_query, b_query, w_kv, b_kv, k_cache, v_cache)
        m = ml[:2 * heads, :batch // 2].reshape(2, heads, batch // 2).transpose(2, 0, 1).reshape(batch, heads, 1)
        l = ml[2 * heads:, :batch // 2].reshape(2, heads, batch // 2).transpose(2, 0, 1).reshape(batch, heads, 1)
        top = lax.pmax(m, "sq")
        f = jnp.exp(m - top)
        num, den = lax.psum((acc.reshape(batch, heads, dim) * f, l * f), "sq")
        attended = (num / den).astype(BF16).reshape(batch, heads * dim)
        rows = batch // mesh.shape["sq"]
        mine = lax.dynamic_slice_in_dim(attended, lax.axis_index("sq") * rows, rows, 0)
        part = jnp.dot(mine, w_out, preferred_element_type=F32)
        total = lax.psum(part, "tp")
        gathered = lax.all_gather(total, "sq", axis=0, tiled=True)
        out_hidden = (hidden.astype(F32) + gathered + b_out).astype(BF16)
        return out_hidden, key_new, val_new

    cache_spec = P("dp", "sq", None)
    row_spec = P("dp", None)
    in_specs = (row_spec, P("dp"), cache_spec, cache_spec, P(None), P(None), P(None, "tp"), P("tp"), P(None, None), P(None), P("tp", None), P(None))
    out_specs = (row_spec, cache_spec, cache_spec)
    return jax.shard_map(local_step, mesh=mesh, in_specs=in_specs, out_specs=out_specs, check_vma=False)
```

time: 207 us -> 161 us (0.78)
  Pallas kernels: 0 us -> 26.1 us
  other arithmetic: 31.7 us -> 6.46 us
  matrix products: 24.8 us -> 1.28 us
  waiting for transfers between devices: 107 us -> 84.7 us
    psum x2, waiting for transfers between devices: 107 us -> 61.1 us  [the longest x1 38.8 us: local_step(): total = lax.psum(part, 'tp')]
    pallas_call x0 -> x1, Pallas kernels: none -> 26.1 us  [attend(): pl.pallas_call(functools.partial(attend_kernel, pairs), out_shape=(jax.Sh...]
    all_gather x0 -> x1, waiting for transfers between devices: none -> 23.6 us  [local_step(): gathered = lax.all_gather(total, 'sq', axis=0, tiled=True)]
    dot_general x5 -> x1, matrix products: 24.8 us -> 1.28 us  [local_step(): part = jnp.dot(mine, w_out, preferred_element_type=F32)]
    select_n x1 -> x0, other arithmetic: 23.3 us -> none  [local_step(): key_new = jnp.where(at_slot, key_val[:, None, :head_dim], k_cache)]
    reduce_sum x3 -> x0, other arithmetic: 4.01 us -> none  [the longest x1 1.64 us: layer_norm(): variance = jnp.mean(centered * centered, axis=-1, keepdims=True)]
    mul x0 -> x1, other arithmetic: none -> 2.17 us  [local_step(): num, den = lax.psum((acc.reshape(batch, heads, dim) * f, l * f), 'sq')]
  transfers between devices with their start and end apart: 2 -> 3, of which waited for: 2 -> 3; matrix products, arithmetic and copies ran while one was open for 0% -> 0% of each run, Pallas kernels for 0% -> 0%
where the time goes in v1:
time: 161 us; the launch traced here: 160 us
  waiting for transfers between devices  84.7 us (53%)
  blocking collectives  26.5 us (16%)
  Pallas kernels  26.1 us (16%)
  between operations  13.8 us (9%)
  other arithmetic  6.46 us (4%)
    psum x1, waiting for transfers between devices, local_step(): total = lax.psum(part, 'tp')  38.8 us
    pallas_call x1, Pallas kernels, attend(): pl.pallas_call(functools.partial(attend_kernel, pairs), out_shape=(jax.Sh...  26.1 us
    all_gather x1, waiting for transfers between devices, local_step(): gathered = lax.all_gather(total, 'sq', axis=0, tiled=True)  23.6 us
    psum x1, waiting for transfers between devices, local_step(): num, den = lax.psum((acc.reshape(batch, heads, dim) * f, l * f), 'sq')  22.3 us
    pmax x1, blocking collectives, local_step(): top = lax.pmax(m, 'sq')  14.5 us
    psum x1, blocking collectives, local_step(): num, den = lax.psum((acc.reshape(batch, heads, dim) * f, l * f), 'sq')  12 us
  transfers between devices with their start and end apart: 3, of which 3 were waited for; matrix products, arithmetic and copies ran while one was open for 0% of the time, Pallas kernels for 0%

profile of v1, /device:TPU:0, one launch (start us, length us, event | category | flops | bytes accessed | tf_op | source)
XLA Modules:
  0.0 160.2 jit_solution(8033315636019931758)
XLA Ops:
  7.2 0.0 copy-start
  7.2 0.0 all-reduce.3.cloned.1.call-start
  7.2 26.1 %attend.1 = (bf16[256,256,128]{2,1,0:T(8,128)(2,1)}, bf16[256,256,128]{2,1,0:T(8,128)(2,1)}, f32[1024,128]{1,0:T(8,128)}, f32[16,128]{1,0:T(8,128)}) custom-call(s32[256]{0:T(256)} %lens_ref.1, bf16[256,2048]{1,0:T(8,128)(2,1)} %x_hbm.1, f32[1,2048]{1,0:T(1,128)} %bitcast.37, f32[1,2048]{1,0:T(1,128)} %bitcast.38, bf16[2048,512]{1,0:T(8,128)(2,1)} %wq_hbm.1, ...), custom_call_target="tpu_custom_call" | custom-call | flops 2147483648 | bytes 75497472 | tf_op jit(solution)/shard_map/attend/pallas_call | solution.py:168
  33.4 0.7 fusion.5
  34.1 0.2 copy.15
  34.2 0.2 copy.16
  34.4 14.5 %pmax.7 = f32[256,4,1]{1,0,2:T(8,128)S(1)} all-reduce(f32[256,4,1]{1,0,2:T(8,128)S(1)} %bitcast.29), channel_id=1, replica_groups=mesh['dp'=2,'tp'=4,'sq'=4] {'sq'}, use_global_device_ids=true, to_apply=%region_0.0 | all-reduce | flops 1024 | bytes 8192 | tf_op jit(solution)/shard_map/pmax | solution.py:204
  48.9 2.2 %broadcast_multiply_fusion = f32[256,4,128]{2,1,0:T(4,128)} fusion(f32[256,4,128]{2,1,0:T(4,128)} %bitcast.33, f32[256,4]{1,0:T(8,128)S(1)} %get-tuple-element.12), kind=kLoop, calls=%fused_computation.3 | loop fusion | flops 131072 | bytes 1052672 | tf_op jit(solution)/shard_map/mul | solution.py:206
  51.1 0.0 all-reduce.3.cloned.1.call-update
  51.1 0.0 all-reduce.5.cloned.1.call-start
  51.2 12.0 %psum.22 = f32[256,4]{1,0:T(8,128)S(1)} all-reduce(f32[256,4]{1,0:T(8,128)S(1)} %get-tuple-element.11), channel_id=1, replica_groups=mesh['dp'=2,'tp'=4,'sq'=4] {'sq'}, use_global_device_ids=true, to_apply=%region_2.0 | all-reduce | flops 1024 | bytes 8192 | tf_op jit(solution)/shard_map/psum | solution.py:206
  63.2 22.3 %all-reduce.3.cloned.1.call-done = f32[256,4,128]{2,1,0:T(4,128)} async-done(((f32[256,4,128]{2,1,0:T(4,128)}), f32[256,4,128]{2,1,0:T(4,128)}) %all-reduce.3.cloned.1.call-update) | async-done | bytes 524304 | tf_op jit(solution)/shard_map/psum | solution.py:206
  85.5 1.4 divide_convert_fusion
  86.9 0.0 copy-start.1
  86.9 0.0 copy-start.2
  87.0 0.0 copy-done
  87.0 1.3 fusion.1
  88.3 0.0 all-reduce.5.cloned.1.call-update
  88.3 0.0 all-gather.2.cloned.1.call-start
  88.4 38.8 %all-reduce.5.cloned.1.call-done = f32[64,2048]{1,0:T(8,128)} async-done(((f32[64,2048]{1,0:T(8,128)}), f32[64,2048]{1,0:T(8,128)}) %all-reduce.5.cloned.1.call-update) | async-done | bytes 524304 | tf_op jit(solution)/shard_map/psum | solution.py:211
  127.1 0.0 all-gather.2.cloned.1.call-update
  127.1 23.6 %all-gather.2.cloned.1.call-done = f32[256,2048]{1,0:T(8,128)} async-done(((f32[64,2048]{1,0:T(8,128)}), f32[256,2048]{1,0:T(8,128)}) %all-gather.2.cloned.1.call-update) | async-done | bytes 2097168 | tf_op jit(solution)/shard_map/all_gather | solution.py:212
  150.8 0.0 copy-done.1
  150.8 0.0 copy-done.2
  150.8 2.9 %add_convert_fusion = bf16[256,2048]{1,0:T(8,128)(2,1)} fusion(f32[256,2048]{1,0:T(8,128)} %all-gather.2.cloned.1.call-done, bf16[256,2048]{1,0:T(8,128)(2,1)S(1)} %copy-done.1, f32[2048]{0:T(1024)S(1)} %copy-done.2), kind=kLoop, calls=%fused_computation | loop fusion | flops 2097152 | bytes 4202496 | tf_op jit(solution)/shard_map/convert_element_type | solution.py:213
  (2 shorter events, 0.1 us)
Async XLA Ops:
  7.2 79.8 %copy-start = (bf16[512,2048]{1,0:T(8,128)(2,1)S(1)}, bf16[512,2048]{1,0:T(8,128)(2,1)}, u32[]{:S(2)}) copy-start(bf16[512,2048]{1,0:T(8,128)(2,1)} %param.22) | copy-start | bytes 6291460
  7.2 78.4 %all-reduce.3.cloned.1.call-start = ((), (), s32[]{:S(2)}) async-start(), calls=%async_computation | async-start | bytes 1048576 | tf_op jit(solution)/shard_map/psum | solution.py:206
  51.1 76.0 %all-reduce.5.cloned.1.call-start = ((), (), s32[]{:S(2)}) async-start(), calls=%async_computation.1 | async-start | bytes 1048576 | tf_op jit(solution)/shard_map/psum | solution.py:211
  86.9 63.8 %copy-start.1 = (bf16[256,2048]{1,0:T(8,128)(2,1)S(1)}, bf16[256,2048]{1,0:T(8,128)(2,1)}, u32[]{:S(2)}) copy-start(bf16[256,2048]{1,0:T(8,128)(2,1)} %x_hbm.1) | copy-start | bytes 3145732
  86.9 63.8 %copy-start.2 = (f32[2048]{0:T(1024)S(1)}, f32[2048]{0:T(1024)}, u32[]{:S(2)}) copy-start(f32[2048]{0:T(1024)} %param.23) | copy-start | bytes 24580
  88.3 62.5 %all-gather.2.cloned.1.call-start = ((), (), s32[]{:S(2)}) async-start(), calls=%async_computation.2 | async-start | bytes 2621440 | tf_op jit(solution)/shard_map/all_gather | solution.py:212
Sparse Core Ops, SparseCore 0:
  51.3 34.2 all-reduce.2
  88.5 38.6 all-reduce.4
  128.7 22.0 all-gather.1

commit v2 on v1

--- a/solution.py
+++ b/solution.py
@@ -193,24 +193,193 @@
     )(lens, x, gain.reshape(1, width), bias.reshape(1, width), wq, bq.reshape(1, -1), wkv, bkv.reshape(1, -1), k, v)
 
 
+def meet_kernel(
+    parts, acc_ref, ml_ref, x_hbm, wo_ref, bo_ref, out_ref,
+    x_buf, sq_buf, ml_buf, a_buf, z_out, z_in, y_buf, x_sem,
+    ml_send, ml_recv, sq_send, sq_recv, z_send, z_recv, g_send, g_recv, y_send, y_recv, c_send, c_recv, f_send, f_recv,
+):
+    n_sq, n_tp = sq_buf.shape[0] + 1, z_in.shape[0] + 1
+    width = y_buf.shape[1]
+    dim = acc_ref.shape[1]
+    sq, tp = lax.axis_index("sq"), lax.axis_index("tp")
+    own = y_buf.shape[0] // n_sq
+    step = own // parts
+    cols = width // n_tp
+    heads = wo_ref.shape[0] // dim
+    rows = 2 * heads
+    pairs = step // 2
+    fold = step * heads
+    mesh_id = pl.DeviceIdType.MESH
+
+    def at_sq(d):
+        return {"sq": lax.rem(sq + d, n_sq)}
+
+    def at_tp(d):
+        return {"tp": lax.rem(tp + d, n_tp)}
+
+    core = {"sq": sq + 1 - 2 * lax.rem(sq, 2)}
+    across = {"sq": lax.rem(sq + 2, n_sq)}
+    core_sq = sq + 1 - 2 * lax.rem(sq, 2)
+    across_sq = lax.rem(sq + 2, n_sq)
+
+    x_copy = pltpu.make_async_copy(x_hbm.at[pl.ds(pl.multiple_of(sq * own, own), own), pl.ds(pl.multiple_of(tp * cols, cols), cols)], x_buf, x_sem)
+    x_copy.start()
+
+    barrier = pltpu.get_barrier_semaphore()
+    for d in range(1, n_sq):
+        pl.semaphore_signal(barrier, inc=1, device_id=at_sq(d), device_id_type=mesh_id)
+    for d in range(1, n_tp):
+        pl.semaphore_signal(barrier, inc=1, device_id=at_tp(d), device_id_type=mesh_id)
+    pl.semaphore_wait(barrier, n_sq - 1 + n_tp - 1)
+
+    def remote(src, dst, send, recv, to):
+        return pltpu.make_async_remote_copy(src_ref=src, dst_ref=dst, send_sem=send, recv_sem=recv, device_id=to, device_id_type=mesh_id)
+
+    def ml_copy(d):
+        return remote(ml_ref, ml_buf.at[d - 1], ml_send.at[d - 1], ml_recv.at[d - 1], at_sq(d))
+
+    def sq_copy(d, c):
+        start = pl.multiple_of(lax.rem(sq + d, n_sq) * (own * heads) + c * fold, fold)
+        return remote(acc_ref.at[pl.ds(start, fold)], sq_buf.at[d - 1, pl.ds(c * fold, fold)], sq_send.at[d - 1, c], sq_recv.at[d - 1, c], at_sq(d))
+
+    def z_copy(d, c):
+        return remote(z_out.at[d - 1, c], z_in.at[d - 1, c], z_send.at[d - 1, c], z_recv.at[d - 1, c], at_tp(d))
+
+    def rows_of(s, c):
+        return pl.ds(pl.multiple_of(s * own + c * step, step), step)
+
+    my_cols = pl.ds(pl.multiple_of(tp * cols, cols), cols)
+
+    def g_copy(d, c):
+        block = y_buf.at[rows_of(sq, c), my_cols]
+        return remote(block, block, g_send.at[d - 1, c], g_recv.at[d - 1, c], at_tp(d))
+
+    def y_copy(c):
+        block = y_buf.at[rows_of(sq, c)]
+        return remote(block, block, y_send.at[c], y_recv.at[c], across)
+
+    def c_copy(c):
+        block = y_buf.at[rows_of(sq, c)]
+        return remote(block, block, c_send.at[c], c_recv.at[c], core)
+
+    def f_copy(c):
+        block = y_buf.at[rows_of(across_sq, c)]
+        return remote(block, block, f_send.at[c], f_recv.at[c], core)
+
+    for d in range(1, n_sq):
+        ml_copy(d).start()
+    for c in range(parts):
+        for d in range(1, n_sq):
+            sq_copy(d, c).start()
+    x_copy.wait()
+
+    for d in range(1, n_sq):
+        ml_copy(d).wait()
+    maxima = [ml_ref[:rows, :]] + [ml_buf[d, :rows, :] for d in range(n_sq - 1)]
+    sums = [ml_ref[rows:, :]] + [ml_buf[d, rows:, :] for d in range(n_sq - 1)]
+    top = functools.reduce(jnp.maximum, maxima)
+    scales = [jnp.exp(m - top) for m in maxima]
+    den = sum(e * s for e, s in zip(scales, sums))
+    scales = [e / den for e in scales]
+    lane = lax.broadcasted_iota(jnp.int32, (rows, dim), 1)
+
+    def project(c):
+        for d in range(1, n_sq):
+            sq_copy(d, c).wait()
+        for j in range(pairs):
+            p = sq * (own // 2) + c * pairs + j
+            pick = lane == p
+            mine = pl.multiple_of(sq * (own * heads) + c * fold + j * rows, rows)
+            terms = [acc_ref[pl.ds(mine, rows), :]]
+            terms += [sq_buf[d, c * fold + j * rows:c * fold + (j + 1) * rows, :] for d in range(n_sq - 1)]
+            total = sum(jnp.sum(jnp.where(pick, e, 0.0), axis=1, keepdims=True) * t for e, t in zip(scales, terms))
+            a_buf[j * rows:(j + 1) * rows, :] = total
+        lhs = jnp.concatenate([a_buf[pl.ds(n, step, stride=heads), :].astype(BF16) for n in range(heads)], axis=1)
+        for d in list(range(1, n_tp)) + [0]:
+            to = lax.rem(tp + d, n_tp)
+            w = wo_ref[:, pl.ds(pl.multiple_of(to * cols, cols), cols)]
+            z_out[(d - 1) % n_tp, c] = jnp.dot(lhs, w, preferred_element_type=F32)
+            if d:
+                z_copy(d, c).start()
+
+    def finish(c):
+        for d in range(1, n_tp):
+            z_copy(d, c).wait()
+        total = z_out[n_tp - 1, c] + sum(z_in[d, c] for d in range(n_tp - 1))
+        total = total + x_buf[c * step:(c + 1) * step, :].astype(F32) + bo_ref[:, my_cols]
+        y_buf[rows_of(sq, c), my_cols] = total
+        for d in range(1, n_tp):
+            g_copy(d, c).start()
+
+    def spread(c):
+        for d in range(1, n_tp):
+            g_copy(d, c).wait()
+        y_copy(c).start()
+        c_copy(c).start()
+
+    def forward(c):
+        y_copy(c).wait()
+        f_copy(c).start()
+
+    def emit(s, c):
+        out_ref[rows_of(s, c), :] = y_buf[rows_of(s, c), :].astype(BF16)
+
+    def collect(c):
+        emit(sq, c)
+        emit(across_sq, c)
+        c_copy(c).wait()
+        emit(core_sq, c)
+        f_copy(c).wait()
+        emit(lax.rem(core_sq + 2, n_sq), c)
+
+    stages = (project, finish, spread, forward, collect)
+    for tick in range(parts + len(stages) - 1):
+        for k, stage in enumerate(stages):
+            if 0 <= tick - k < parts:
+                stage(tick - k)
+
+
+def meet(acc, ml, x, wo, bo, n_sq, n_tp, parts=4):
+    batch, width = x.shape
+    own = batch // n_sq
+    cols = width // n_tp
+    step = own // parts
+    heads = wo.shape[0] // acc.shape[1]
+    dim = acc.shape[1]
+    hbm = pl.BlockSpec(memory_space=pl.ANY)
+    vmem = pl.BlockSpec(memory_space=pltpu.VMEM)
+    dma = pltpu.SemaphoreType.DMA
+    return pl.pallas_call(
+        functools.partial(meet_kernel, parts),
+        out_shape=jax.ShapeDtypeStruct((batch, width), BF16),
+        in_specs=[vmem, vmem, hbm, vmem, vmem],
+        out_specs=vmem,
+        scratch_shapes=[
+            pltpu.VMEM((own, cols), BF16),
+            pltpu.VMEM((n_sq - 1, own * heads, dim), F32),
+            pltpu.VMEM((n_sq - 1,) + ml.shape, F32),
+            pltpu.VMEM((step * heads, dim), F32),
+            pltpu.VMEM((n_tp, parts, step, cols), F32),
+            pltpu.VMEM((n_tp - 1, parts, step, cols), F32),
+            pltpu.VMEM((batch, width), F32),
+            dma,
+            dma((n_sq - 1,)), dma((n_sq - 1,)),
+            dma((n_sq - 1, parts)), dma((n_sq - 1, parts)),
+            dma((n_tp - 1, parts)), dma((n_tp - 1, parts)),
+            dma((n_tp - 1, parts)), dma((n_tp - 1, parts)),
+            dma((parts,)), dma((parts,)), dma((parts,)), dma((parts,)), dma((parts,)), dma((parts,)),
+        ],
+        compiler_params=pltpu.CompilerParams(collective_id=0, has_side_effects=True, vmem_limit_bytes=24 * 1024 * 1024),
+        cost_estimate=pl.CostEstimate(flops=2**28, bytes_accessed=8 * 2**20, transcendentals=0),
+        name="meet",
+    )(acc, ml, x, wo, bo.reshape(1, width))
+
+
 def solution(mesh):
     def local_step(hidden, cache_lens, k_cache, v_cache, ln_gain, ln_bias, w_query, b_query, w_kv, b_kv, w_out, b_out):
-        batch, pos_local, dim = k_cache.shape
-        heads = w_query.shape[1] // dim
         key_new, val_new, acc, ml = attend(
             cache_lens, hidden, ln_gain, ln_bias, w_query, b_query, w_kv, b_kv, k_cache, v_cache)
-        m = ml[:2 * heads, :batch // 2].reshape(2, heads, batch // 2).transpose(2, 0, 1).reshape(batch, heads, 1)
-        l = ml[2 * heads:, :batch // 2].reshape(2, heads, batch // 2).transpose(2, 0, 1).reshape(batch, heads, 1)
-        top = lax.pmax(m, "sq")
-        f = jnp.exp(m - top)
-        num, den = lax.psum((acc.reshape(batch, heads, dim) * f, l * f), "sq")
-        attended = (num / den).astype(BF16).reshape(batch, heads * dim)
-        rows = batch // mesh.shape["sq"]
-        mine = lax.dynamic_slice_in_dim(attended, lax.axis_index("sq") * rows, rows, 0)
-        part = jnp.dot(mine, w_out, preferred_element_type=F32)
-        total = lax.psum(part, "tp")
-        gathered = lax.all_gather(total, "sq", axis=0, tiled=True)
-        out_hidden = (hidden.astype(F32) + gathered + b_out).astype(BF16)
+        out_hidden = meet(acc, ml, hidden, w_out, b_out, mesh.shape["sq"], mesh.shape["tp"])
         return out_hidden, key_new, val_new
 
     cache_spec = P("dp", "sq", None)

time: 161 us -> 71.6 us (0.44)
  waiting for transfers between devices: 84.7 us -> 0 us
  Pallas kernels: 26.1 us -> 68 us
  blocking collectives: 26.5 us -> 0 us
  between operations: 13.8 us -> 0.71 us
  other arithmetic: 6.46 us -> 0 us
  local copies, waits for them, and re-layouts: 1.05 us -> 2.72 us
    psum x2 -> x0, waiting for transfers between devices: 61.1 us -> none  [the longest x1 38.8 us: local_step(): total = lax.psum(part, 'tp')]
    pallas_call x0 -> x1, Pallas kernels: none -> 41.8 us  [meet(): pl.pallas_call(functools.partial(meet_kernel, parts), out_shape=jax.Shape...]
    all_gather x1 -> x0, waiting for transfers between devices: 23.6 us -> none  [local_step(): gathered = lax.all_gather(total, 'sq', axis=0, tiled=True)]
    pmax x1 -> x0, blocking collectives: 14.5 us -> none  [local_step(): top = lax.pmax(m, 'sq')]
    psum x1 -> x0, blocking collectives: 12 us -> none  [local_step(): num, den = lax.psum((acc.reshape(batch, heads, dim) * f, l * f), 'sq')]
    convert_element_type x2 -> x0, other arithmetic: 4.25 us -> none  [the longest x1 2.87 us: local_step(): out_hidden = (hidden.astype(F32) + gathered + b_out).astype(BF16)]
    unnamed x7 -> x11, local copies, waits for them, and re-layouts: 0.06 us -> 2.72 us
    mul x1 -> x0, other arithmetic: 2.17 us -> none  [local_step(): num, den = lax.psum((acc.reshape(batch, heads, dim) * f, l * f), 'sq')]
  transfers between devices with their start and end apart: 3 -> 0, of which waited for: 3 -> 0; matrix products, arithmetic and copies ran while one was open for 0% -> 0% of each run, Pallas kernels for 0% -> 0%
where the time goes in v2:
time: 71.6 us; the launch traced here: 71.4 us
  Pallas kernels  68 us (95%)
  local copies, waits for them, and re-layouts  2.72 us (4%)
    pallas_call x1, Pallas kernels, meet(): pl.pallas_call(functools.partial(meet_kernel, parts), out_shape=jax.Shape...  41.8 us
    pallas_call x1, Pallas kernels, attend(): pl.pallas_call(functools.partial(attend_kernel, pairs), out_shape=(jax.Sh...  26.2 us
    unnamed x11, local copies, waits for them, and re-layouts  2.72 us

profile of v2, /device:TPU:0, one launch (start us, length us, event | category | flops | bytes accessed | tf_op | source)
XLA Modules:
  0.0 71.4 jit_solution(6087317557934648517)
XLA Ops:
  0.6 0.0 copy-start
  0.6 0.0 copy-start.1
  0.7 0.0 copy-start.3
  0.7 26.2 %attend.1 = (bf16[256,256,128]{2,1,0:T(8,128)(2,1)}, bf16[256,256,128]{2,1,0:T(8,128)(2,1)}, f32[1024,128]{1,0:T(8,128)}, f32[16,128]{1,0:T(8,128)}) custom-call(s32[256]{0:T(256)} %lens_ref.1, bf16[256,2048]{1,0:T(8,128)(2,1)} %x_hbm.3, f32[1,2048]{1,0:T(1,128)} %bitcast.6, f32[1,2048]{1,0:T(1,128)} %bitcast.7, bf16[2048,512]{1,0:T(8,128)(2,1)} %wq_hbm.1, ...), custom_call_target="tpu_custom_call" | custom-call | flops 2147483648 | bytes 75497472 | tf_op jit(solution)/shard_map/attend/pallas_call | solution.py:168
  26.9 0.0 copy-done
  26.9 0.0 copy-done.1
  26.9 0.0 copy-done.3
  26.9 0.0 copy-start.2
  26.9 1.0 %copy-done.2 = f32[1024,128]{1,0:T(8,128)S(1)} copy-done((f32[1024,128]{1,0:T(8,128)S(1)}, f32[1024,128]{1,0:T(8,128)}, u32[]{:S(2)}) %copy-start.2) | copy-done | bytes 524312
  27.9 0.0 copy-start.4
  27.9 0.7 copy-done.4
  28.6 41.8 %meet.1 = bf16[256,2048]{1,0:T(8,128)(2,1)S(1)} custom-call(f32[1024,128]{1,0:T(8,128)S(1)} %copy-done.2, f32[16,128]{1,0:T(8,128)S(1)} %copy-done.4, bf16[256,2048]{1,0:T(8,128)(2,1)S(1)} %copy-done, bf16[512,2048]{1,0:T(8,128)(2,1)S(1)} %copy-done.1, f32[1,2048]{1,0:T(1,128)S(1)} %bitcast.5), custom_call_target="tpu_custom_call" | custom-call | flops 268435456 | bytes 8388608 | tf_op jit(solution)/shard_map/meet/pallas_call | solution.py:352
  70.4 1.0 %copy.16 = bf16[256,2048]{1,0:T(8,128)(2,1)} copy(bf16[256,2048]{1,0:T(8,128)(2,1)S(1)} %meet.1) | data formatting | bytes 2097152
Async XLA Ops:
  0.6 26.2 %copy-start = (bf16[256,2048]{1,0:T(8,128)(2,1)S(1)}, bf16[256,2048]{1,0:T(8,128)(2,1)}, u32[]{:S(2)}) copy-start(bf16[256,2048]{1,0:T(8,128)(2,1)} %x_hbm.3) | copy-start | bytes 3145732
  0.6 26.2 %copy-start.1 = (bf16[512,2048]{1,0:T(8,128)(2,1)S(1)}, bf16[512,2048]{1,0:T(8,128)(2,1)}, u32[]{:S(2)}) copy-start(bf16[512,2048]{1,0:T(8,128)(2,1)} %wo_ref.1) | copy-start | bytes 6291460
  0.7 26.2 %copy-start.3 = (f32[2048]{0:T(1024)S(1)}, f32[2048]{0:T(1024)}, u32[]{:S(2)}) copy-start(f32[2048]{0:T(1024)} %param.23) | copy-start | bytes 24580
  26.9 1.0 %copy-start.2 = (f32[1024,128]{1,0:T(8,128)S(1)}, f32[1024,128]{1,0:T(8,128)}, u32[]{:S(2)}) copy-start(f32[1024,128]{1,0:T(8,128)} %get-tuple-element.7.acc_ref) | copy-start | bytes 1572868
  27.9 0.7 copy-start.4

commit v3 on v2

--- a/solution.py
+++ b/solution.py
@@ -13,9 +13,10 @@
 
 
 def attend_kernel(
-    pairs, lens_ref, x_hbm, gain_ref, bias_ref, wq_hbm, bq_ref, wkv_hbm, bkv_ref, k_hbm, v_hbm,
-    k_out, v_out, acc_ref, ml_ref,
-    x_buf, h_buf, wq_buf, wkv_buf, q_buf, kv_buf, s_buf, k_buf, v_buf, in_sem, k_sem, v_sem, ko_sem, vo_sem,
+    pairs, held, lens_ref, x_hbm, gain_ref, bias_ref, wq_hbm, bq_ref, wkv_hbm, bkv_ref, k_hbm, v_hbm,
+    k_out, v_out, acc_out, ml_out,
+    x_buf, h_buf, wq_buf, wkv_buf, q_buf, kv_buf, s_buf, acc_ref, ml_ref, k_buf, v_buf,
+    in_sem, k_sem, v_sem, ko_sem, vo_sem, acc_sem, ml_sem,
 ):
     batch, pos_local, dim = k_buf.shape
     heads = wq_buf.shape[1] // dim
@@ -125,48 +126,79 @@
         for j, s in enumerate(out):
             s_buf[j * rows:(j + 1) * rows, :] = s
 
-    def arrive(c):
+    def acc_store(c):
+        part = pl.ds(pl.multiple_of(c * (pairs * rows), pairs * rows), pairs * rows)
+        return pltpu.make_async_copy(acc_ref.at[part], acc_out.at[part], acc_sem.at[c])
+
+    def loaded(c):
         k_load(c).wait()
         v_load(c).wait()
-        update_rows(c)
 
     def leave(c):
         k_store(c).start()
         v_store(c).start()
 
-    arrive(0)
+    loaded(0)
+    update_rows(0)
     put_scores(score(0))
-    leave(0)
     zero = jnp.zeros((rows, dim), F32)
 
-    def body(c, carry):
-        arrive(c + 1)
+    def early(c, carry):
+        loaded(c + 1)
+        update_rows(c + 1)
         carry = weigh(c, *carry)
         put_scores(score(c + 1))
+        acc_store(c).start()
+        return carry
+
+    carry = lax.fori_loop(0, held, early, (zero, zero))
+
+    @pl.loop(held + 1, chunks)
+    def _(c):
+        loaded(c)
+
+    @pl.loop(0, held + 1)
+    def _(c):
+        leave(c)
+
+    def late(c, carry):
+        update_rows(c + 1)
+        carry = weigh(c, *carry)
+        put_scores(score(c + 1))
+        acc_store(c).start()
         leave(c + 1)
         return carry
 
-    carry = lax.fori_loop(0, chunks - 1, body, (zero, zero))
+    carry = lax.fori_loop(held, chunks - 1, late, carry)
     m_all, l_all = weigh(chunks - 1, *carry)
     ml_ref[:rows, :] = m_all
     ml_ref[rows:, :] = l_all
-
-    @pl.loop(0, chunks)
+    acc_store(chunks - 1).start()
+
+    @pl.loop(0, chunks - 1)
     def _(c):
         k_store(c).wait()
         v_store(c).wait()
-
-
-def attend(lens, x, gain, bias, wq, bq, wkv, bkv, k, v, pairs=8):
+        acc_store(c).wait()
+
+    ml_store = pltpu.make_async_copy(ml_ref, ml_out, ml_sem)
+    ml_store.start()
+    k_store(chunks - 1).wait()
+    v_store(chunks - 1).wait()
+    acc_store(chunks - 1).wait()
+    ml_store.wait()
+
+
+def attend(lens, x, gain, bias, wq, bq, wkv, bkv, k, v, pairs=8, held=8):
     batch, pos_local, dim = k.shape
     width = x.shape[1]
     heads = wq.shape[1] // dim
     chunks = batch // (2 * pairs)
-    hbm = pl.BlockSpec(memory_space=pl.ANY)
+    hbm = pl.BlockSpec(memory_space=pltpu.HBM)
     vmem = pl.BlockSpec(memory_space=pltpu.VMEM)
     dma = pltpu.SemaphoreType.DMA
     return pl.pallas_call(
-        functools.partial(attend_kernel, pairs),
+        functools.partial(attend_kernel, pairs, held),
         out_shape=(
             jax.ShapeDtypeStruct(k.shape, k.dtype),
             jax.ShapeDtypeStruct(v.shape, v.dtype),
@@ -174,7 +206,7 @@
             jax.ShapeDtypeStruct((4 * heads, dim), F32),
         ),
         in_specs=[pl.BlockSpec(memory_space=pltpu.SMEM), hbm, vmem, vmem, hbm, vmem, hbm, vmem, hbm, hbm],
-        out_specs=(hbm, hbm, vmem, vmem),
+        out_specs=(hbm, hbm, hbm, hbm),
         scratch_shapes=[
             pltpu.VMEM(x.shape, BF16),
             pltpu.VMEM(x.shape, BF16),
@@ -183,24 +215,27 @@
             pltpu.VMEM((batch * heads, dim), F32),
             pltpu.VMEM((batch, 2 * dim), F32),
             pltpu.VMEM((pairs * 2 * heads, pos_local), F32),
+            pltpu.VMEM((batch * heads, dim), F32),
+            pltpu.VMEM((4 * heads, dim), F32),
             pltpu.VMEM(k.shape, BF16),
             pltpu.VMEM(v.shape, BF16),
-            dma((3,)), dma((chunks,)), dma((chunks,)), dma((chunks,)), dma((chunks,)),
+            dma((3,)), dma((chunks,)), dma((chunks,)), dma((chunks,)), dma((chunks,)), dma((chunks,)), dma,
         ],
-        compiler_params=pltpu.CompilerParams(vmem_limit_bytes=56 * 1024 * 1024),
+        compiler_params=pltpu.CompilerParams(vmem_limit_bytes=60 * 1024 * 1024),
         cost_estimate=pl.CostEstimate(flops=2 * 2**30, bytes_accessed=72 * 2**20, transcendentals=0),
         name="attend",
     )(lens, x, gain.reshape(1, width), bias.reshape(1, width), wq, bq.reshape(1, -1), wkv, bkv.reshape(1, -1), k, v)
 
 
 def meet_kernel(
-    parts, acc_ref, ml_ref, x_hbm, wo_ref, bo_ref, out_ref,
-    x_buf, sq_buf, ml_buf, a_buf, z_out, z_in, y_buf, x_sem,
-    ml_send, ml_recv, sq_send, sq_recv, z_send, z_recv, g_send, g_recv, y_send, y_recv, c_send, c_recv, f_send, f_recv,
+    parts, timing, acc_hbm, ml_hbm, x_hbm, wo_hbm, bo_ref, out_ref,
+    wo_ref, acc_buf, ml_own, x_buf, base_buf, sq_buf, ml_buf, a_buf, z_out, z_in, y_buf, in_sem,
+    ml_send, ml_recv, sq_send, sq_recv, z_send, z_recv, l_send, l_recv, r_send, r_recv,
+    y_send, y_recv, c_send, c_recv, f_send, f_recv,
 ):
     n_sq, n_tp = sq_buf.shape[0] + 1, z_in.shape[0] + 1
     width = y_buf.shape[1]
-    dim = acc_ref.shape[1]
+    dim = acc_buf.shape[1]
     sq, tp = lax.axis_index("sq"), lax.axis_index("tp")
     own = y_buf.shape[0] // n_sq
     step = own // parts
@@ -217,66 +252,90 @@
     def at_tp(d):
         return {"tp": lax.rem(tp + d, n_tp)}
 
-    core = {"sq": sq + 1 - 2 * lax.rem(sq, 2)}
-    across = {"sq": lax.rem(sq + 2, n_sq)}
     core_sq = sq + 1 - 2 * lax.rem(sq, 2)
     across_sq = lax.rem(sq + 2, n_sq)
-
-    x_copy = pltpu.make_async_copy(x_hbm.at[pl.ds(pl.multiple_of(sq * own, own), own), pl.ds(pl.multiple_of(tp * cols, cols), cols)], x_buf, x_sem)
-    x_copy.start()
+    core, across = {"sq": core_sq}, {"sq": across_sq}
+
+    x_cols = pl.ds(pl.multiple_of(tp * cols, cols), cols)
+    ml_in = pltpu.make_async_copy(ml_hbm, ml_own, in_sem.at[0])
+    acc_in = pltpu.make_async_copy(acc_hbm, acc_buf, in_sem.at[1])
+    x_in = pltpu.make_async_copy(x_hbm.at[pl.ds(pl.multiple_of(sq * own, own), own), x_cols], x_buf, in_sem.at[2])
+    wo_in = pltpu.make_async_copy(wo_hbm, wo_ref, in_sem.at[3])
+    ml_in.start()
+    acc_in.start()
+    x_in.start()
+    wo_in.start()
 
     barrier = pltpu.get_barrier_semaphore()
     for d in range(1, n_sq):
         pl.semaphore_signal(barrier, inc=1, device_id=at_sq(d), device_id_type=mesh_id)
     for d in range(1, n_tp):
         pl.semaphore_signal(barrier, inc=1, device_id=at_tp(d), device_id_type=mesh_id)
+    ml_in.wait()
+    acc_in.wait()
     pl.semaphore_wait(barrier, n_sq - 1 + n_tp - 1)
 
     def remote(src, dst, send, recv, to):
         return pltpu.make_async_remote_copy(src_ref=src, dst_ref=dst, send_sem=send, recv_sem=recv, device_id=to, device_id_type=mesh_id)
 
     def ml_copy(d):
-        return remote(ml_ref, ml_buf.at[d - 1], ml_send.at[d - 1], ml_recv.at[d - 1], at_sq(d))
+        return remote(ml_own, ml_buf.at[d - 1], ml_send.at[d - 1], ml_recv.at[d - 1], at_sq(d))
 
     def sq_copy(d, c):
         start = pl.multiple_of(lax.rem(sq + d, n_sq) * (own * heads) + c * fold, fold)
-        return remote(acc_ref.at[pl.ds(start, fold)], sq_buf.at[d - 1, pl.ds(c * fold, fold)], sq_send.at[d - 1, c], sq_recv.at[d - 1, c], at_sq(d))
+        return remote(acc_buf.at[pl.ds(start, fold)], sq_buf.at[d - 1, pl.ds(c * fold, fold)], sq_send.at[d - 1, c], sq_recv.at[d - 1, c], at_sq(d))
 
     def z_copy(d, c):
         return remote(z_out.at[d - 1, c], z_in.at[d - 1, c], z_send.at[d - 1, c], z_recv.at[d - 1, c], at_tp(d))
 
-    def rows_of(s, c):
-        return pl.ds(pl.multiple_of(s * own + c * step, step), step)
-
-    my_cols = pl.ds(pl.multiple_of(tp * cols, cols), cols)
-
-    def g_copy(d, c):
-        block = y_buf.at[rows_of(sq, c), my_cols]
-        return remote(block, block, g_send.at[d - 1, c], g_recv.at[d - 1, c], at_tp(d))
-
-    def y_copy(c):
-        block = y_buf.at[rows_of(sq, c)]
-        return remote(block, block, y_send.at[c], y_recv.at[c], across)
-
-    def c_copy(c):
-        block = y_buf.at[rows_of(sq, c)]
-        return remote(block, block, c_send.at[c], c_recv.at[c], core)
-
-    def f_copy(c):
-        block = y_buf.at[rows_of(across_sq, c)]
-        return remote(block, block, f_send.at[c], f_recv.at[c], core)
+    def block(s, t, c):
+        return y_buf.at[pl.ds(pl.multiple_of(s * own + c * step, step), step), pl.ds(pl.multiple_of(t * cols, cols), cols)]
+
+    def source(tag):
+        return tp - tag if tag < n_tp else tp + (tag - n_tp + 1)
+
+    def right_copy(tag, c):
+        b = block(sq, source(tag), c)
+        return remote(b, b, l_send.at[tag, c], l_recv.at[tag + 1, c], {"tp": tp + 1})
+
+    def left_copy(tag, c):
+        b = block(sq, source(tag), c)
+        hop = tag if tag == 0 else tag - n_tp + 1
+        return remote(b, b, r_send.at[hop, c], r_recv.at[hop + 1, c], {"tp": tp - 1})
+
+    def from_left(hop, c):
+        b = block(sq, tp - hop, c)
+        return remote(b, b, l_send.at[hop, c], l_recv.at[hop, c], {"tp": tp})
+
+    def from_right(hop, c):
+        b = block(sq, tp + hop, c)
+        return remote(b, b, r_send.at[hop, c], r_recv.at[hop, c], {"tp": tp})
+
+    def y_copy(tag, c):
+        b = block(sq, source(tag), c)
+        return remote(b, b, y_send.at[tag, c], y_recv.at[tag, c], across)
+
+    def c_copy(tag, c):
+        b = block(sq, source(tag), c)
+        return remote(b, b, c_send.at[tag, c], c_recv.at[tag, c], core)
+
+    def f_copy(tag, c):
+        b = block(across_sq, source(tag), c)
+        return remote(b, b, f_send.at[tag, c], f_recv.at[tag, c], core)
 
     for d in range(1, n_sq):
         ml_copy(d).start()
     for c in range(parts):
         for d in range(1, n_sq):
             sq_copy(d, c).start()
-    x_copy.wait()
+    x_in.wait()
+    wo_in.wait()
+    base_buf[...] = x_buf[...].astype(F32) + bo_ref[:, x_cols]
 
     for d in range(1, n_sq):
         ml_copy(d).wait()
-    maxima = [ml_ref[:rows, :]] + [ml_buf[d, :rows, :] for d in range(n_sq - 1)]
-    sums = [ml_ref[rows:, :]] + [ml_buf[d, rows:, :] for d in range(n_sq - 1)]
+    maxima = [ml_own[:rows, :]] + [ml_buf[d, :rows, :] for d in range(n_sq - 1)]
+    sums = [ml_own[rows:, :]] + [ml_buf[d, rows:, :] for d in range(n_sq - 1)]
     top = functools.reduce(jnp.maximum, maxima)
     scales = [jnp.exp(m - top) for m in maxima]
     den = sum(e * s for e, s in zip(scales, sums))
@@ -290,7 +349,7 @@
             p = sq * (own // 2) + c * pairs + j
             pick = lane == p
             mine = pl.multiple_of(sq * (own * heads) + c * fold + j * rows, rows)
-            terms = [acc_ref[pl.ds(mine, rows), :]]
+            terms = [acc_buf[pl.ds(mine, rows), :]]
             terms += [sq_buf[d, c * fold + j * rows:c * fold + (j + 1) * rows, :] for d in range(n_sq - 1)]
             total = sum(jnp.sum(jnp.where(pick, e, 0.0), axis=1, keepdims=True) * t for e, t in zip(scales, terms))
             a_buf[j * rows:(j + 1) * rows, :] = total
@@ -302,74 +361,159 @@
             if d:
                 z_copy(d, c).start()
 
+    def share(tag, c):
+        y_copy(tag, c).start()
+        c_copy(tag, c).start()
+
+    def when(cond):
+        return pl.when(cond)
+
     def finish(c):
         for d in range(1, n_tp):
             z_copy(d, c).wait()
         total = z_out[n_tp - 1, c] + sum(z_in[d, c] for d in range(n_tp - 1))
-        total = total + x_buf[c * step:(c + 1) * step, :].astype(F32) + bo_ref[:, my_cols]
-        y_buf[rows_of(sq, c), my_cols] = total
-        for d in range(1, n_tp):
-            g_copy(d, c).start()
-
-    def spread(c):
-        for d in range(1, n_tp):
-            g_copy(d, c).wait()
-        y_copy(c).start()
-        c_copy(c).start()
-
-    def forward(c):
-        y_copy(c).wait()
-        f_copy(c).start()
-
-    def emit(s, c):
-        out_ref[rows_of(s, c), :] = y_buf[rows_of(s, c), :].astype(BF16)
-
-    def collect(c):
-        emit(sq, c)
-        emit(across_sq, c)
-        c_copy(c).wait()
-        emit(core_sq, c)
-        f_copy(c).wait()
-        emit(lax.rem(core_sq + 2, n_sq), c)
-
-    stages = (project, finish, spread, forward, collect)
-    for tick in range(parts + len(stages) - 1):
-        for k, stage in enumerate(stages):
-            if 0 <= tick - k < parts:
-                stage(tick - k)
-
-
-def meet(acc, ml, x, wo, bo, n_sq, n_tp, parts=4):
+        total = total + base_buf[c * step:(c + 1) * step, :]
+        mine = block(sq, tp, c)
+        mine[...] = total
+
+        @when(tp < n_tp - 1)
+        def _():
+            right_copy(0, c).start()
+
+        @when(tp > 0)
+        def _():
+            left_copy(0, c).start()
+
+        share(0, c)
+
+    def hop(h, c):
+        @when(tp >= h)
+        def _():
+            from_left(h, c).wait_recv()
+
+            @when(tp < n_tp - 1)
+            def _():
+                right_copy(h, c).start()
+
+            share(h, c)
+
+        @when(tp + h < n_tp)
+        def _():
+            from_right(h, c).wait_recv()
+
+            @when(tp > 0)
+            def _():
+                left_copy(h + n_tp - 1, c).start()
+
+            share(h + n_tp - 1, c)
+
+    def crossed(h, c):
+        def take(tag):
+            y_copy(tag, c).wait_recv()
+            f_copy(tag, c).start()
+
+        if h == 0:
+            take(0)
+            return
+
+        @when(tp >= h)
+        def _():
+            take(h)
+
+        @when(tp + h < n_tp)
+        def _():
+            take(h + n_tp - 1)
+
+    tau, lag, leg = timing
+    events = []
+    for c in range(parts):
+        t = c * tau
+        events.append((t, 0, functools.partial(project, c)))
+        t += lag
+        events.append((t, 1, functools.partial(finish, c)))
+        events.append((t + leg, 3, functools.partial(crossed, 0, c)))
+        for h in range(1, n_tp):
+            events.append((t + h * leg, 2, functools.partial(hop, h, c)))
+            events.append((t + (h + 1) * leg, 3, functools.partial(crossed, h, c)))
+    for _, _, event in sorted(events, key=lambda e: e[:2]):
+        event()
+
+    def close(tag, c):
+        y_copy(tag, c).wait_send()
+        c_copy(tag, c).wait()
+        f_copy(tag, c).wait()
+
+    for c in range(parts):
+        @when(tp < n_tp - 1)
+        def _():
+            right_copy(0, c).wait_send()
+
+        @when(tp > 0)
+        def _():
+            left_copy(0, c).wait_send()
+
+        close(0, c)
+        for h in range(1, n_tp):
+            @when(tp >= h)
+            def _():
+                @when(tp < n_tp - 1)
+                def _():
+                    right_copy(h, c).wait_send()
+
+                close(h, c)
+
+            @when(tp + h < n_tp)
+            def _():
+                @when(tp > 0)
+                def _():
+                    left_copy(h + n_tp - 1, c).wait_send()
+
+                close(h + n_tp - 1, c)
+
+    chunk = 32
+    for i in range(y_buf.shape[0] // chunk):
+        out_ref[i * chunk:(i + 1) * chunk, :] = y_buf[i * chunk:(i + 1) * chunk, :].astype(BF16)
+
+
+def meet(acc, ml, x, wo, bo, n_sq, n_tp, parts=8, timing=(1.4, 4.0, 2.5)):
     batch, width = x.shape
     own = batch // n_sq
     cols = width // n_tp
     step = own // parts
     heads = wo.shape[0] // acc.shape[1]
     dim = acc.shape[1]
-    hbm = pl.BlockSpec(memory_space=pl.ANY)
+    hbm = pl.BlockSpec(memory_space=pltpu.HBM)
     vmem = pl.BlockSpec(memory_space=pltpu.VMEM)
     dma = pltpu.SemaphoreType.DMA
+    tags = 2 * n_tp - 1
     return pl.pallas_call(
-        functools.partial(meet_kernel, parts),
+        functools.partial(meet_kernel, parts, timing),
         out_shape=jax.ShapeDtypeStruct((batch, width), BF16),
-        in_specs=[vmem, vmem, hbm, vmem, vmem],
+        in_specs=[hbm, hbm, hbm, hbm, vmem],
         out_specs=vmem,
         scratch_shapes=[
+            pltpu.VMEM(wo.shape, BF16),
+            pltpu.VMEM(acc.shape, F32),
+            pltpu.VMEM(ml.shape, F32),
             pltpu.VMEM((own, cols), BF16),
+            pltpu.VMEM((own, cols), F32),
             pltpu.VMEM((n_sq - 1, own * heads, dim), F32),
             pltpu.VMEM((n_sq - 1,) + ml.shape, F32),
             pltpu.VMEM((step * heads, dim), F32),
             pltpu.VMEM((n_tp, parts, step, cols), F32),
             pltpu.VMEM((n_tp - 1, parts, step, cols), F32),
             pltpu.VMEM((batch, width), F32),
-            dma,
+            dma((4,)),
             dma((n_sq - 1,)), dma((n_sq - 1,)),
             dma((n_sq - 1, parts)), dma((n_sq - 1, parts)),
             dma((n_tp - 1, parts)), dma((n_tp - 1, parts)),
-            dma((n_tp - 1, parts)), dma((n_tp - 1, parts)),
-            dma((parts,)), dma((parts,)), dma((parts,)), dma((parts,)), dma((parts,)), dma((parts,)),
+            dma((n_tp + 1, parts)), dma((n_tp + 1, parts)),
+            dma((n_tp + 1, parts)), dma((n_tp + 1, parts)),
+            dma((tags, parts)), dma((tags, parts)),
+            dma((tags, parts)), dma((tags, parts)),
+            dma((tags, parts)), dma((tags, parts)),
         ],
-        compiler_params=pltpu.CompilerParams(collective_id=0, has_side_effects=True, vmem_limit_bytes=24 * 1024 * 1024),
+        compiler_params=pltpu.CompilerParams(collective_id=0, has_side_effects=True, vmem_limit_bytes=60 * 1024 * 1024),
         cost_estimate=pl.CostEstimate(flops=2**28, bytes_accessed=8 * 2**20, transcendentals=0),
         name="meet",
     )(acc, ml, x, wo, bo.reshape(1, width))

time: 71.6 us -> 73.7 us (1.029)
  Pallas kernels: 68 us -> 70.4 us
    pallas_call x2, Pallas kernels: 68 us -> 70.4 us  [the longest x1 45.5 us: meet(): pl.pallas_call(functools.partial(meet_kernel, parts, timing), out_shape=j...]
    unnamed x11 -> x1, local copies, waits for them, and re-layouts: 2.72 us -> 2.3 us
where the time goes in v3:
time: 73.7 us; the launch traced here: 73.4 us
  Pallas kernels  70.4 us (96%)
  local copies, waits for them, and re-layouts  2.3 us (3%)
    pallas_call x1, Pallas kernels, meet(): pl.pallas_call(functools.partial(meet_kernel, parts, timing), out_shape=j...  45.5 us
    pallas_call x1, Pallas kernels, attend(): pl.pallas_call(functools.partial(attend_kernel, pairs, held), out_shape=(...  24.9 us
    unnamed x1, local copies, waits for them, and re-layouts  2.3 us

profile of v3, /device:TPU:0, one launch (start us, length us, event | category | flops | bytes accessed | tf_op | source)
XLA Modules:
  0.0 73.4 jit_solution(12666740096081381583)
XLA Ops:
  0.6 24.9 %attend.1 = (bf16[256,256,128]{2,1,0:T(8,128)(2,1)}, bf16[256,256,128]{2,1,0:T(8,128)(2,1)}, f32[1024,128]{1,0:T(8,128)}, f32[16,128]{1,0:T(8,128)}) custom-call(s32[256]{0:T(256)} %lens_ref.1, bf16[256,2048]{1,0:T(8,128)(2,1)} %x_hbm.3, f32[1,2048]{1,0:T(1,128)} %bitcast.5, f32[1,2048]{1,0:T(1,128)} %bitcast.6, bf16[2048,512]{1,0:T(8,128)(2,1)} %wq_hbm.1, ...), custom_call_target="tpu_custom_call" | custom-call | flops 2147483648 | bytes 75497472 | tf_op jit(solution)/shard_map/attend/pallas_call | solution.py:200
  25.6 45.5 %meet.1 = bf16[256,2048]{1,0:T(8,128)(2,1)} custom-call(f32[1024,128]{1,0:T(8,128)} %get-tuple-element.7.acc_hbm, f32[16,128]{1,0:T(8,128)} %get-tuple-element.8.ml_hbm, bf16[256,2048]{1,0:T(8,128)(2,1)} %x_hbm.3, bf16[512,2048]{1,0:T(8,128)(2,1)} %wo_hbm.1, f32[1,2048]{1,0:T(1,128)} %bitcast.7), custom_call_target="tpu_custom_call" | custom-call | flops 268435456 | bytes 8388608 | tf_op jit(solution)/shard_map/meet/pallas_call | solution.py:489
  71.1 2.3 %copy.16 = bf16[256,2048]{1,0:T(8,128)(2,1)} copy(bf16[256,2048]{1,0:T(8,128)(2,1)} %meet.1) | data formatting | bytes 2097152

commit v4 on v3

--- a/solution.py
+++ b/solution.py
@@ -228,9 +228,9 @@
 
 
 def meet_kernel(
-    parts, timing, acc_hbm, ml_hbm, x_hbm, wo_hbm, bo_ref, out_ref,
-    wo_ref, acc_buf, ml_own, x_buf, base_buf, sq_buf, ml_buf, a_buf, z_out, z_in, y_buf, in_sem,
-    ml_send, ml_recv, sq_send, sq_recv, z_send, z_recv, l_send, l_recv, r_send, r_recv,
+    parts, relayed, acc_hbm, ml_hbm, x_hbm, wo_hbm, bo_hbm, out_ref,
+    wo_ref, bo_ref, acc_buf, ml_own, x_buf, base_buf, sq_buf, ml_buf, a_buf, z_out, z_in, y_buf, in_sem,
+    ml_send, ml_recv, sq_send, sq_recv, z_send, z_recv, g_send, g_recv, l_send, l_recv, r_send, r_recv,
     y_send, y_recv, c_send, c_recv, f_send, f_recv,
 ):
     n_sq, n_tp = sq_buf.shape[0] + 1, z_in.shape[0] + 1
@@ -256,21 +256,23 @@
     across_sq = lax.rem(sq + 2, n_sq)
     core, across = {"sq": core_sq}, {"sq": across_sq}
 
+    barrier = pltpu.get_barrier_semaphore()
+    for d in range(1, n_sq):
+        pl.semaphore_signal(barrier, inc=1, device_id=at_sq(d), device_id_type=mesh_id)
+    for d in range(1, n_tp):
+        pl.semaphore_signal(barrier, inc=1, device_id=at_tp(d), device_id_type=mesh_id)
     x_cols = pl.ds(pl.multiple_of(tp * cols, cols), cols)
     ml_in = pltpu.make_async_copy(ml_hbm, ml_own, in_sem.at[0])
     acc_in = pltpu.make_async_copy(acc_hbm, acc_buf, in_sem.at[1])
     x_in = pltpu.make_async_copy(x_hbm.at[pl.ds(pl.multiple_of(sq * own, own), own), x_cols], x_buf, in_sem.at[2])
     wo_in = pltpu.make_async_copy(wo_hbm, wo_ref, in_sem.at[3])
+    bo_in = pltpu.make_async_copy(bo_hbm.at[:, x_cols], bo_ref, in_sem.at[4])
     ml_in.start()
     acc_in.start()
     x_in.start()
+    bo_in.start()
     wo_in.start()
 
-    barrier = pltpu.get_barrier_semaphore()
-    for d in range(1, n_sq):
-        pl.semaphore_signal(barrier, inc=1, device_id=at_sq(d), device_id_type=mesh_id)
-    for d in range(1, n_tp):
-        pl.semaphore_signal(barrier, inc=1, device_id=at_tp(d), device_id_type=mesh_id)
     ml_in.wait()
     acc_in.wait()
     pl.semaphore_wait(barrier, n_sq - 1 + n_tp - 1)
@@ -311,16 +313,23 @@
         b = block(sq, tp + hop, c)
         return remote(b, b, r_send.at[hop, c], r_recv.at[hop, c], {"tp": tp})
 
+    def source_of(tag, c):
+        return source(tag) if c < relayed else lax.rem(tp - tag + n_tp, n_tp)
+
+    def g_copy(d, c):
+        b = block(sq, tp, c)
+        return remote(b, b, g_send.at[d - 1, c], g_recv.at[d - 1, c], at_tp(d))
+
     def y_copy(tag, c):
-        b = block(sq, source(tag), c)
+        b = block(sq, source_of(tag, c), c)
         return remote(b, b, y_send.at[tag, c], y_recv.at[tag, c], across)
 
     def c_copy(tag, c):
-        b = block(sq, source(tag), c)
+        b = block(sq, source_of(tag, c), c)
         return remote(b, b, c_send.at[tag, c], c_recv.at[tag, c], core)
 
     def f_copy(tag, c):
-        b = block(across_sq, source(tag), c)
+        b = block(across_sq, source_of(tag, c), c)
         return remote(b, b, f_send.at[tag, c], f_recv.at[tag, c], core)
 
     for d in range(1, n_sq):
@@ -330,7 +339,8 @@
             sq_copy(d, c).start()
     x_in.wait()
     wo_in.wait()
-    base_buf[...] = x_buf[...].astype(F32) + bo_ref[:, x_cols]
+    bo_in.wait()
+    base_buf[...] = x_buf[...].astype(F32) + bo_ref[...]
 
     for d in range(1, n_sq):
         ml_copy(d).wait()
@@ -358,8 +368,8 @@
             to = lax.rem(tp + d, n_tp)
             w = wo_ref[:, pl.ds(pl.multiple_of(to * cols, cols), cols)]
             z_out[(d - 1) % n_tp, c] = jnp.dot(lhs, w, preferred_element_type=F32)
-            if d:
-                z_copy(d, c).start()
+        for d in range(1, n_tp):
+            z_copy(d, c).start()
 
     def share(tag, c):
         y_copy(tag, c).start()
@@ -376,15 +386,23 @@
         mine = block(sq, tp, c)
         mine[...] = total
 
-        @when(tp < n_tp - 1)
-        def _():
-            right_copy(0, c).start()
-
-        @when(tp > 0)
-        def _():
-            left_copy(0, c).start()
+        if c < relayed:
+            @when(tp < n_tp - 1)
+            def _():
+                right_copy(0, c).start()
+
+            @when(tp > 0)
+            def _():
+                left_copy(0, c).start()
+        else:
+            for d in range(1, n_tp):
+                g_copy(d, c).start()
 
         share(0, c)
+
+    def direct(d, c):
+        g_copy(d, c).wait_recv()
+        share(d, c)
 
     def hop(h, c):
         @when(tp >= h)
@@ -412,8 +430,8 @@
             y_copy(tag, c).wait_recv()
             f_copy(tag, c).start()
 
-        if h == 0:
-            take(0)
+        if h == 0 or c >= relayed:
+            take(h)
             return
 
         @when(tp >= h)
@@ -424,17 +442,21 @@
         def _():
             take(h + n_tp - 1)
 
-    tau, lag, leg = timing
+    slow = 11.2 / parts
     events = []
     for c in range(parts):
-        t = c * tau
-        events.append((t, 0, functools.partial(project, c)))
-        t += lag
+        events.append((6.3 + 5.6 / parts * c, 0, functools.partial(project, c)))
+        t = 9.3 + slow * (c + 1)
         events.append((t, 1, functools.partial(finish, c)))
-        events.append((t + leg, 3, functools.partial(crossed, 0, c)))
+        events.append((t + 2.7, 3, functools.partial(crossed, 0, c)))
         for h in range(1, n_tp):
-            events.append((t + h * leg, 2, functools.partial(hop, h, c)))
-            events.append((t + (h + 1) * leg, 3, functools.partial(crossed, h, c)))
+            if c < relayed:
+                there = t + 3.0 * h
+                events.append((there, 2, functools.partial(hop, h, c)))
+            else:
+                there = t + (4.0 if h == 2 else 3.0) + 0.5 * h
+                events.append((there, 2, functools.partial(direct, h, c)))
+            events.append((there + 2.7, 3, functools.partial(crossed, h, c)))
     for _, _, event in sorted(events, key=lambda e: e[:2]):
         event()
 
@@ -444,6 +466,13 @@
         f_copy(tag, c).wait()
 
     for c in range(parts):
+        close(0, c)
+        if c >= relayed:
+            for d in range(1, n_tp):
+                g_copy(d, c).wait_send()
+                close(d, c)
+            continue
+
         @when(tp < n_tp - 1)
         def _():
             right_copy(0, c).wait_send()
@@ -452,7 +481,6 @@
         def _():
             left_copy(0, c).wait_send()
 
-        close(0, c)
         for h in range(1, n_tp):
             @when(tp >= h)
             def _():
@@ -475,7 +503,7 @@
         out_ref[i * chunk:(i + 1) * chunk, :] = y_buf[i * chunk:(i + 1) * chunk, :].astype(BF16)
 
 
-def meet(acc, ml, x, wo, bo, n_sq, n_tp, parts=8, timing=(1.4, 4.0, 2.5)):
+def meet(acc, ml, x, wo, bo, n_sq, n_tp, parts=4, relayed=2):
     batch, width = x.shape
     own = batch // n_sq
     cols = width // n_tp
@@ -487,12 +515,13 @@
     dma = pltpu.SemaphoreType.DMA
     tags = 2 * n_tp - 1
     return pl.pallas_call(
-        functools.partial(meet_kernel, parts, timing),
+        functools.partial(meet_kernel, parts, relayed),
         out_shape=jax.ShapeDtypeStruct((batch, width), BF16),
-        in_specs=[hbm, hbm, hbm, hbm, vmem],
+        in_specs=[hbm, hbm, hbm, hbm, hbm],
         out_specs=vmem,
         scratch_shapes=[
             pltpu.VMEM(wo.shape, BF16),
+            pltpu.VMEM((1, cols), F32),
             pltpu.VMEM(acc.shape, F32),
             pltpu.VMEM(ml.shape, F32),
             pltpu.VMEM((own, cols), BF16),
@@ -503,9 +532,10 @@
             pltpu.VMEM((n_tp, parts, step, cols), F32),
             pltpu.VMEM((n_tp - 1, parts, step, cols), F32),
             pltpu.VMEM((batch, width), F32),
-            dma((4,)),
+            dma((5,)),
             dma((n_sq - 1,)), dma((n_sq - 1,)),
             dma((n_sq - 1, parts)), dma((n_sq - 1, parts)),
+            dma((n_tp - 1, parts)), dma((n_tp - 1, parts)),
             dma((n_tp - 1, parts)), dma((n_tp - 1, parts)),
             dma((n_tp + 1, parts)), dma((n_tp + 1, parts)),
             dma((n_tp + 1, parts)), dma((n_tp + 1, parts)),

time: 73.7 us -> 73.8 us (level)
  no operation moved by 1% of the time
where the time goes in v4:
time: 73.8 us; the launch traced here: 73.6 us
  Pallas kernels  70.6 us (96%)
  local copies, waits for them, and re-layouts  2.3 us (3%)
    pallas_call x1, Pallas kernels, meet(): pl.pallas_call(functools.partial(meet_kernel, parts, relayed), out_shape=...  45.7 us
    pallas_call x1, Pallas kernels, attend(): pl.pallas_call(functools.partial(attend_kernel, pairs, held), out_shape=(...  24.9 us
    unnamed x1, local copies, waits for them, and re-layouts  2.3 us

profile of v4, /device:TPU:0, one launch (start us, length us, event | category | flops | bytes accessed | tf_op | source)
XLA Modules:
  0.0 73.6 jit_solution(16808107266966264633)
XLA Ops:
  0.6 24.9 %attend.1 = (bf16[256,256,128]{2,1,0:T(8,128)(2,1)}, bf16[256,256,128]{2,1,0:T(8,128)(2,1)}, f32[1024,128]{1,0:T(8,128)}, f32[16,128]{1,0:T(8,128)}) custom-call(s32[256]{0:T(256)} %lens_ref.1, bf16[256,2048]{1,0:T(8,128)(2,1)} %x_hbm.3, f32[1,2048]{1,0:T(1,128)} %bitcast.5, f32[1,2048]{1,0:T(1,128)} %bitcast.6, bf16[2048,512]{1,0:T(8,128)(2,1)} %wq_hbm.1, ...), custom_call_target="tpu_custom_call" | custom-call | flops 2147483648 | bytes 75497472 | tf_op jit(solution)/shard_map/attend/pallas_call | solution.py:200
  25.6 45.7 %meet.1 = bf16[256,2048]{1,0:T(8,128)(2,1)} custom-call(f32[1024,128]{1,0:T(8,128)} %get-tuple-element.7.acc_hbm, f32[16,128]{1,0:T(8,128)} %get-tuple-element.8.ml_hbm, bf16[256,2048]{1,0:T(8,128)(2,1)} %x_hbm.3, bf16[512,2048]{1,0:T(8,128)(2,1)} %wo_hbm.1, f32[1,2048]{1,0:T(1,128)} %bitcast.7), custom_call_target="tpu_custom_call" | custom-call | flops 268435456 | bytes 8388608 | tf_op jit(solution)/shard_map/meet/pallas_call | solution.py:517
  71.3 2.3 %copy.16 = bf16[256,2048]{1,0:T(8,128)(2,1)} copy(bf16[256,2048]{1,0:T(8,128)(2,1)} %meet.1) | data formatting | bytes 2097152
